TPU v7x, 32 devices: a whole 2x2x4 slice. The times are simulated.
32 devices in a mesh: outer: 4 (over y, x), inner: 8 (over z, core).
Axes of the slice: x: 2, y: 2, z: 4, core: 2. Of those that a mesh axis runs over, the one named last changes fastest.
Arguments:
- queries: bfloat16 [2048, 1024], P(('outer', 'inner')), may hold values from -8 to 8
- key_rows: bfloat16 [2048, 1024], P(('outer', 'inner')), may hold values from -8 to 8
- value_rows: bfloat16 [2048, 1024], P(('outer', 'inner')), may hold values from -6 to 6
Outputs:
- attended: float32 [2048, 1024], P(('outer', 'inner'))
All inputs are finite; a program needn't handle non-finite values.
Results may differ from a plain program's by a relative error of at most 0.0021.
Values may be sent and summed in bfloat16 or wider, within the bound.
A program may use at most 64 MiB of HBM per device.

v0:
```python
from functools import reduce

import jax
import jax.numpy as jnp
import numpy as np
from jax import lax
from jax.sharding import PartitionSpec as P

HEADS = 16


FLOOR_SCORE = -1e30


def divisor_block(length, limit):
    extent = min(length, limit)
    while length % extent:
        extent -= 1
    return extent


def fresh_state(count, rows, width):
    return (
        jnp.full((count, rows), FLOOR_SCORE, jnp.float32),
        jnp.zeros((count, rows), jnp.float32),
        jnp.zeros((count, rows, width), jnp.float32),
    )


def finish_state(state):
    row_max, denominator, summed = state
    return (summed / denominator[..., None], row_max + jnp.log(denominator))


def online_step(state, query_rows, query_rank, key_rows, value_rows, key_rank):
    row_max, denominator, summed = state
    scale = query_rows.shape[-1] ** (-0.5)
    scores = (
        jnp.einsum("inh,ibh->inb", query_rows, key_rows, preferred_element_type=jnp.float32) * scale
    )
    scores = jnp.where(key_rank[None, None, :] <= query_rank[None, :, None], scores, FLOOR_SCORE)
    new_max = jnp.maximum(row_max, jnp.max(scores, axis=2))
    weights = jnp.exp(scores - new_max[..., None])
    rescale = jnp.exp(row_max - new_max)
    denominator = denominator * rescale + jnp.sum(weights, axis=2)
    summed = summed * rescale[..., None] + jnp.einsum(
        "inb,ibh->inh", weights.astype(jnp.bfloat16), value_rows, preferred_element_type=jnp.float32
    )
    return (new_max, denominator, summed)


def attend_keys(state, query_rows, query_rank, key_rows, value_rows, key_rank, stop=None):
    length = key_rows.shape[1]
    block = divisor_block(length, 512)

    def advance(index, carry):
        start = index * block
        piece_keys = lax.dynamic_slice_in_dim(key_rows, start, block, 1)
        piece_values = lax.dynamic_slice_in_dim(value_rows, start, block, 1)
        piece_rank = lax.dynamic_slice_in_dim(key_rank, start, block, 0)
        return online_step(carry, query_rows, query_rank, piece_keys, piece_values, piece_rank)

    upper = length // block if stop is None else stop
    return lax.fori_loop(0, upper, advance, state)


def attend(query_rows, query_rank, key_rows, value_rows, key_rank):
    count, length, width = query_rows.shape
    block = divisor_block(length, 512)
    steps = length // block
    query_split = query_rows.reshape(count, steps, block, width).swapaxes(0, 1)
    rank_split = query_rank.reshape(steps, block)

    def one_block(pieces):
        state = attend_keys(
            fresh_state(count, block, width),
            pieces[0],
            pieces[1],
            key_rows,
            value_rows,
            key_rank,
            pieces[2] + 1,
        )
        return finish_state(state)

    outputs, lses = lax.map(
        one_block, (query_split, rank_split, jnp.arange(steps, dtype=jnp.int32))
    )
    return (
        outputs.swapaxes(0, 1).reshape(count, length, width),
        lses.swapaxes(0, 1).reshape(count, length),
    )


def merge_levels(parts):
    row_max = reduce(jnp.maximum, [lse for _, lse in parts])
    weights = [jnp.exp(lse - row_max) for _, lse in parts]
    denominator = reduce(jnp.add, weights)
    summed = reduce(
        jnp.add, [weight[..., None] * output for weight, (output, _) in zip(weights, parts)]
    )
    return (summed / denominator[..., None], row_max + jnp.log(denominator))


def on_device(queries, key_rows, value_rows):
    tokens, features = queries.shape
    heads = HEADS
    width = features // heads
    outer_count = lax.axis_size("outer")
    inner_count = lax.axis_size("inner")
    outer_index = lax.axis_index("outer")
    inner_index = lax.axis_index("inner")
    per_device = 4 * heads // inner_count
    quarter = tokens // 4
    sixteenth = tokens // 16
    class_len = quarter * inner_count
    far_len = sixteenth * inner_count

    def to_items(array):
        return (
            array.reshape(quarter, 4, heads, width)
            .transpose(2, 1, 0, 3)
            .reshape(4 * heads, quarter, width)
        )

    local_ranks = jnp.arange(tokens, dtype=jnp.int32)
    head_major = [
        a.reshape(tokens, heads, width).transpose(1, 0, 2) for a in (queries, key_rows, value_rows)
    ]
    near_out, near_lse = attend(
        head_major[0], local_ranks, head_major[1], head_major[2], local_ranks
    )
    near_out = near_out.transpose(1, 0, 2)
    near_lse = near_lse.T
    item_index = inner_index * per_device + jnp.arange(per_device, dtype=jnp.int32)
    band = item_index // 16
    far_query_rank = outer_index * far_len + jnp.arange(far_len, dtype=jnp.int32)
    pick = np.array(
        [head * 16 + head // 4 * 4 + residue for head in range(heads) for residue in range(4)],
        np.int32,
    )

    def to_sixteen(array):
        spread = (
            array.reshape(sixteenth, 16, heads, width)
            .transpose(2, 1, 0, 3)
            .reshape(16 * heads, sixteenth, width)
        )
        return jnp.take(spread, pick, axis=0)

    gathered_k, gathered_v = (
        lax.all_gather(to_sixteen(key_rows), "outer", axis=1, tiled=True),
        lax.all_gather(to_sixteen(value_rows), "outer", axis=1, tiled=True),
    )
    mid_q, mid_k, mid_v, far_k, far_v = (
        lax.all_to_all(to_items(queries), "inner", split_axis=0, concat_axis=1, tiled=True),
        lax.all_to_all(to_items(key_rows), "inner", split_axis=0, concat_axis=1, tiled=True),
        lax.all_to_all(to_items(value_rows), "inner", split_axis=0, concat_axis=1, tiled=True),
        lax.all_to_all(gathered_k, "inner", split_axis=0, concat_axis=1, tiled=True),
        lax.all_to_all(gathered_v, "inner", split_axis=0, concat_axis=1, tiled=True),
    )
    split = mid_q.reshape(per_device, far_len, 4, width)
    picker = jnp.broadcast_to(band[:, None, None, None], (per_device, far_len, 1, width))
    far_q = jnp.take_along_axis(split, picker, axis=2)[:, :, 0, :]
    position = jnp.arange(far_k.shape[1], dtype=jnp.int32)
    far_key_rank = (
        position // sixteenth % outer_count * far_len
        + position // (outer_count * sixteenth) * sixteenth
        + position % sixteenth
    )
    far_state = attend_keys(
        fresh_state(per_device, far_len, width), far_q, far_query_rank, far_k, far_v, far_key_rank
    )
    far_out, far_lse = finish_state(far_state)
    class_ranks = jnp.arange(class_len, dtype=jnp.int32)
    mid_out, mid_lse = attend(mid_q, class_ranks, mid_k, mid_v, class_ranks)
    back_mid, back_mid_lse, back_far, back_far_lse = (
        lax.all_to_all(mid_out, "inner", split_axis=1, concat_axis=0, tiled=True),
        lax.all_to_all(mid_lse, "inner", split_axis=1, concat_axis=0, tiled=True),
        lax.all_to_all(far_out, "inner", split_axis=1, concat_axis=0, tiled=True),
        lax.all_to_all(far_lse, "inner", split_axis=1, concat_axis=0, tiled=True),
    )
    selector = np.array(
        [[band_index == head // 4 for band_index in range(4)] for head in range(heads)]
    )
    spread_out = jnp.where(
        selector[:, :, None, None, None], back_far.reshape(heads, 1, 4, sixteenth, width), 0.0
    )
    spread_lse = jnp.where(
        selector[:, :, None, None], back_far_lse.reshape(heads, 1, 4, sixteenth), FLOOR_SCORE
    )
    far_placed = (
        spread_out.reshape(heads, 16, sixteenth, width)
        .transpose(2, 1, 0, 3)
        .reshape(tokens, heads, width)
    )
    far_placed_lse = (
        spread_lse.reshape(heads, 16, sixteenth).transpose(2, 1, 0).reshape(tokens, heads)
    )
    placed = (
        back_mid.reshape(heads, 4, quarter, width)
        .transpose(2, 1, 0, 3)
        .reshape(tokens, heads, width)
    )
    placed_lse = back_mid_lse.reshape(heads, 4, quarter).transpose(2, 1, 0).reshape(tokens, heads)
    combined, _ = merge_levels(
        [(near_out, near_lse), (placed, placed_lse), (far_placed, far_placed_lse)]
    )
    return combined.reshape(tokens, features)


def solution(mesh):
    placed = (P(("outer", "inner"), None), P(("outer", "inner"), None), P(("outer", "inner"), None))
    return jax.shard_map(
        on_device,
        mesh=mesh,
        in_specs=placed,
        out_specs=P(("outer", "inner"), None),
        check_vma=False,
    )
```

profile of v0, /device:TPU:0, one launch (start us, length us, event | category | flops | bytes accessed | tf_op | source)
XLA Modules:
  0.0 281.8 jit_solution(14643228419734093072)
XLA Ops:
  0.0 1.1 reshape.318
  1.3 0.9 reshape.371
  2.2 6.4 %all-to-all-start = ((bf16[8,2,4096]{2,1,0:T(2,128)(2,1)}), bf16[8,2,4096]{2,1,0:T(2,128)(2,1)S(1)}, u32[]{:S(2)}, u32[]{:S(2)}) async-start(bf16[8,2,4096]{2,1,0:T(2,128)(2,1)} %reshape.371), calls=%async_computation | async-start | bytes 262144 | tf_op jit(solution)/shard_map/all_to_all | solution.py:156
  9.6 0.7 gather_fusion.1
  10.3 9.0 %all_gather.6 = bf16[64,16,64]{2,0,1:T(8,128)(2,1)S(1)} all-gather(bf16[64,4,64]{2,0,1:T(8,128)(2,1)S(1)} %copy.155), channel_id=1, replica_groups=mesh['outer'=4,'inner'=8] {'outer'}, dimensions={1}, use_global_device_ids=true | all-gather | bytes 163840 | tf_op jit(solution)/shard_map/all_gather | solution.py:152
  19.5 0.9 reshape.369
  20.8 0.7 gather_fusion.2
  21.5 0.3 fusion.61
  22.3 5.1 %all-to-all-start.3 = ((bf16[8,2,4096]{2,1,0:T(2,128)(2,1)}), bf16[8,2,4096]{2,1,0:T(2,128)(2,1)S(1)}, u32[]{:S(2)}, u32[]{:S(2)}) async-start(bf16[8,2,4096]{2,1,0:T(2,128)(2,1)} %reshape.369), calls=%async_computation.3 | async-start | bytes 262144 | tf_op jit(solution)/shard_map/all_to_all | solution.py:159
  27.4 9.0 %all_gather.7 = bf16[64,16,64]{2,0,1:T(8,128)(2,1)S(1)} all-gather(bf16[64,4,64]{2,0,1:T(8,128)(2,1)S(1)} %copy.178), channel_id=1, replica_groups=mesh['outer'=4,'inner'=8] {'outer'}, dimensions={1}, use_global_device_ids=true | all-gather | bytes 163840 | tf_op jit(solution)/shard_map/all_gather | solution.py:153
  37.2 0.9 reshape.367
  38.4 0.9 reshape.375
  39.5 0.9 reshape.379
  40.4 0.2 reshape.372
  40.7 164.6 %gather_fusion = bf16[16384]{0:T(1024)(128)(2,1)S(1)} fusion(bf16[8,32,4,64]{3,0,2,1:T(8,128)(2,1)S(1)} %bitcast.125, s32[16384]{0:T(1024)S(1)} %reshape.355), kind=kCustom, calls=%fused_computation.2 | custom fusion | bytes 327680 | tf_op jit(solution)/shard_map/jit(take_along_axis)/gather | solution.py:164
  205.4 5.1 %all-to-all-start.1 = ((bf16[8,2,4096]{2,1,0:T(2,128)(2,1)}), bf16[8,2,4096]{2,1,0:T(2,128)(2,1)S(1)}, u32[]{:S(2)}, u32[]{:S(2)}) async-start(bf16[8,2,4096]{2,1,0:T(2,128)(2,1)} %reshape.375), calls=%async_computation.1 | async-start | bytes 262144 | tf_op jit(solution)/shard_map/all_to_all | solution.py:157
  210.8 0.4 fusion.59
  211.2 6.1 %all-to-all-done.1 = bf16[8,2,4096]{2,1,0:T(2,128)(2,1)S(1)} async-done(((bf16[8,2,4096]{2,1,0:T(2,128)(2,1)}), bf16[8,2,4096]{2,1,0:T(2,128)(2,1)S(1)}, u32[]{:S(2)}, u32[]{:S(2)}) %all-to-all-start.1) | async-done | bytes 131104 | tf_op jit(solution)/shard_map/all_to_all | solution.py:157
  217.3 3.4 %all-to-all-start.7 = ((bf16[8,2,4096]{2,1,0:T(2,128)(2,1)}), bf16[8,2,4096]{2,1,0:T(2,128)(2,1)S(1)}, u32[]{:S(2)}, u32[]{:S(2)}) async-start(bf16[8,2,4096]{2,1,0:T(2,128)(2,1)} %reshape.367), calls=%async_computation.7 | async-start | bytes 262144 | tf_op jit(solution)/shard_map/all_to_all | solution.py:160
  220.7 0.2 reshape.376
  220.9 0.3 fusion.60
  221.5 5.8 %all-to-all-done.7 = bf16[8,2,4096]{2,1,0:T(2,128)(2,1)S(1)} async-done(((bf16[8,2,4096]{2,1,0:T(2,128)(2,1)}), bf16[8,2,4096]{2,1,0:T(2,128)(2,1)S(1)}, u32[]{:S(2)}, u32[]{:S(2)}) %all-to-all-start.7) | async-done | bytes 131104 | tf_op jit(solution)/shard_map/all_to_all | solution.py:160
  227.3 3.4 %all-to-all-start.5 = ((bf16[8,2,4096]{2,1,0:T(2,128)(2,1)}), bf16[8,2,4096]{2,1,0:T(2,128)(2,1)S(1)}, u32[]{:S(2)}, u32[]{:S(2)}) async-start(bf16[8,2,4096]{2,1,0:T(2,128)(2,1)} %reshape.379), calls=%async_computation.5 | async-start | bytes 262144 | tf_op jit(solution)/shard_map/all_to_all | solution.py:158
  231.1 0.6 log_add_fusion
  231.8 5.7 %all-to-all-done.5 = bf16[8,2,4096]{2,1,0:T(2,128)(2,1)S(1)} async-done(((bf16[8,2,4096]{2,1,0:T(2,128)(2,1)}), bf16[8,2,4096]{2,1,0:T(2,128)(2,1)S(1)}, u32[]{:S(2)}, u32[]{:S(2)}) %all-to-all-start.5) | async-done | bytes 131104 | tf_op jit(solution)/shard_map/all_to_all | solution.py:158
  237.4 3.3 %all-to-all-start.4 = ((f32[8,8,4]{0,2,1:T(4,128)}), f32[8,8,4]{0,2,1:T(4,128)S(1)}, u32[]{:S(2)}, u32[]{:S(2)}) async-start(f32[8,8,4]{0,2,1:T(4,128)} %log_add_fusion), calls=%async_computation.4 | async-start | bytes 32768 | tf_op jit(solution)/shard_map/all_to_all | solution.py:181
  240.7 0.2 reshape.380
  241.0 0.2 fusion.8
  241.2 0.2 fusion.9
  241.6 0.7 reshape.373
  242.4 0.7 reshape.377
  243.1 0.2 copy.171
  243.3 1.0 reshape.381
  244.3 2.0 all-to-all-done.4
  246.3 3.3 %all-to-all-start.2 = ((f32[8,1,128]{2,1,0:T(1,128)}), f32[8,1,128]{2,1,0:T(1,128)S(1)}, u32[]{:S(2)}, u32[]{:S(2)}) async-start(f32[8,1,128]{2,1,0:T(1,128)} %reshape.377), calls=%async_computation.2 | async-start | bytes 8192 | tf_op jit(solution)/shard_map/all_to_all | solution.py:179
  249.9 5.2 %all-to-all-done.2 = f32[8,1,128]{2,1,0:T(1,128)S(1)} async-done(((f32[8,1,128]{2,1,0:T(1,128)}), f32[8,1,128]{2,1,0:T(1,128)S(1)}, u32[]{:S(2)}, u32[]{:S(2)}) %all-to-all-start.2) | async-done | bytes 4128 | tf_op jit(solution)/shard_map/all_to_all | solution.py:179
  255.1 3.3 %all-to-all-start.8 = ((f32[8,1,2048]{2,1,0:T(1,128)}), f32[8,1,2048]{2,1,0:T(1,128)S(1)}, u32[]{:S(2)}, u32[]{:S(2)}) async-start(f32[8,1,2048]{2,1,0:T(1,128)} %reshape.373), calls=%async_computation.8 | async-start | bytes 131072 | tf_op jit(solution)/shard_map/all_to_all | solution.py:180
  258.5 0.6 broadcast.515
  259.1 0.7 reduce.1
  260.1 4.3 %all-to-all-done.8 = f32[8,1,2048]{2,1,0:T(1,128)S(1)} async-done(((f32[8,1,2048]{2,1,0:T(1,128)}), f32[8,1,2048]{2,1,0:T(1,128)S(1)}, u32[]{:S(2)}, u32[]{:S(2)}) %all-to-all-start.8) | async-done | bytes 65568 | tf_op jit(solution)/shard_map/all_to_all | solution.py:180
  264.4 3.6 %all-to-all-start.6 = ((f32[8,1,8192]{2,1,0:T(1,128)}), f32[8,1,8192]{2,1,0:T(1,128)S(1)}, u32[]{:S(2)}, u32[]{:S(2)}) async-start(f32[8,1,8192]{2,1,0:T(1,128)} %reshape.381), calls=%async_computation.6 | async-start | bytes 524288 | tf_op jit(solution)/shard_map/all_to_all | solution.py:178
  268.0 0.8 reduce
  269.3 8.1 %all-to-all-done.6 = f32[8,1,8192]{2,1,0:T(1,128)S(1)} async-done(((f32[8,1,8192]{2,1,0:T(1,128)}), f32[8,1,8192]{2,1,0:T(1,128)S(1)}, u32[]{:S(2)}, u32[]{:S(2)}) %all-to-all-start.6) | async-done | bytes 262176 | tf_op jit(solution)/shard_map/all_to_all | solution.py:178
  277.4 1.3 reduce.2
  278.7 0.2 reshape.382
  279.3 1.3 fusion.5
  280.6 0.3 copy.185
  280.9 0.9 reshape.336
  (88 shorter events, 6.1 us)
Async XLA Ops:
  1.1 7.5 %copy-start.2 = (bf16[64,1024]{1,0:T(8,128)(2,1)S(1)}, bf16[64,1024]{1,0:T(8,128)(2,1)}, u32[]{:S(2)}) copy-start(bf16[64,1024]{1,0:T(8,128)(2,1)} %param.8) | copy-start | bytes 393220
  1.3 7.5 %copy-start = (bf16[64,1024]{1,0:T(8,128)(2,1)S(1)}, bf16[64,1024]{1,0:T(8,128)(2,1)}, u32[]{:S(2)}) copy-start(bf16[64,1024]{1,0:T(8,128)(2,1)} %param.9) | copy-start | bytes 393220
  2.2 20.1 %all-to-all-start = ((bf16[8,2,4096]{2,1,0:T(2,128)(2,1)}), bf16[8,2,4096]{2,1,0:T(2,128)(2,1)S(1)}, u32[]{:S(2)}, u32[]{:S(2)}) async-start(bf16[8,2,4096]{2,1,0:T(2,128)(2,1)} %reshape.371), calls=%async_computation | async-start | bytes 262144 | tf_op jit(solution)/shard_map/all_to_all | solution.py:156
  8.7 0.7 copy-start.4
  19.3 1.1 copy-start.1
  22.3 183.1 %all-to-all-start.3 = ((bf16[8,2,4096]{2,1,0:T(2,128)(2,1)}), bf16[8,2,4096]{2,1,0:T(2,128)(2,1)S(1)}, u32[]{:S(2)}, u32[]{:S(2)}) async-start(bf16[8,2,4096]{2,1,0:T(2,128)(2,1)} %reshape.369), calls=%async_computation.3 | async-start | bytes 262144 | tf_op jit(solution)/shard_map/all_to_all | solution.py:159
  36.9 1.2 copy-start.3
  205.4 11.9 %all-to-all-start.1 = ((bf16[8,2,4096]{2,1,0:T(2,128)(2,1)}), bf16[8,2,4096]{2,1,0:T(2,128)(2,1)S(1)}, u32[]{:S(2)}, u32[]{:S(2)}) async-start(bf16[8,2,4096]{2,1,0:T(2,128)(2,1)} %reshape.375), calls=%async_computation.1 | async-start | bytes 262144 | tf_op jit(solution)/shard_map/all_to_all | solution.py:157
  217.3 10.1 %all-to-all-start.7 = ((bf16[8,2,4096]{2,1,0:T(2,128)(2,1)}), bf16[8,2,4096]{2,1,0:T(2,128)(2,1)S(1)}, u32[]{:S(2)}, u32[]{:S(2)}) async-start(bf16[8,2,4096]{2,1,0:T(2,128)(2,1)} %reshape.367), calls=%async_computation.7 | async-start | bytes 262144 | tf_op jit(solution)/shard_map/all_to_all | solution.py:160
  227.3 10.1 %all-to-all-start.5 = ((bf16[8,2,4096]{2,1,0:T(2,128)(2,1)}), bf16[8,2,4096]{2,1,0:T(2,128)(2,1)S(1)}, u32[]{:S(2)}, u32[]{:S(2)}) async-start(bf16[8,2,4096]{2,1,0:T(2,128)(2,1)} %reshape.379), calls=%async_computation.5 | async-start | bytes 262144 | tf_op jit(solution)/shard_map/all_to_all | solution.py:158
  237.4 8.9 %all-to-all-start.4 = ((f32[8,8,4]{0,2,1:T(4,128)}), f32[8,8,4]{0,2,1:T(4,128)S(1)}, u32[]{:S(2)}, u32[]{:S(2)}) async-start(f32[8,8,4]{0,2,1:T(4,128)} %log_add_fusion), calls=%async_computation.4 | async-start | bytes 32768 | tf_op jit(solution)/shard_map/all_to_all | solution.py:181
  246.3 8.8 %all-to-all-start.2 = ((f32[8,1,128]{2,1,0:T(1,128)}), f32[8,1,128]{2,1,0:T(1,128)S(1)}, u32[]{:S(2)}, u32[]{:S(2)}) async-start(f32[8,1,128]{2,1,0:T(1,128)} %reshape.377), calls=%async_computation.2 | async-start | bytes 8192 | tf_op jit(solution)/shard_map/all_to_all | solution.py:179
  255.1 9.2 %all-to-all-start.8 = ((f32[8,1,2048]{2,1,0:T(1,128)}), f32[8,1,2048]{2,1,0:T(1,128)S(1)}, u32[]{:S(2)}, u32[]{:S(2)}) async-start(f32[8,1,2048]{2,1,0:T(1,128)} %reshape.373), calls=%async_computation.8 | async-start | bytes 131072 | tf_op jit(solution)/shard_map/all_to_all | solution.py:180
  264.4 13.1 %all-to-all-start.6 = ((f32[8,1,8192]{2,1,0:T(1,128)}), f32[8,1,8192]{2,1,0:T(1,128)S(1)}, u32[]{:S(2)}, u32[]{:S(2)}) async-start(f32[8,1,8192]{2,1,0:T(1,128)} %reshape.381), calls=%async_computation.6 | async-start | bytes 524288 | tf_op jit(solution)/shard_map/all_to_all | solution.py:178
where the time goes:
time: 283 us; the launch traced here: 282 us
  local copies, waits for them, and re-layouts  182 us (64%)
  waiting for transfers between devices  37.1 us (13%)
  starting transfers between devices  36.9 us (13%)
  blocking collectives  17.9 us (6%)
  other arithmetic  4.61 us (2%)
    gather x3, local copies, waits for them, and re-layouts, on_device(): far_q = jnp.take_along_axis(split, picker, axis=2)[:, :, 0, :]  165 us
    all_gather x1, blocking collectives, on_device(): lax.all_gather(to_sixteen(key_rows), 'outer', axis=1, tiled=True)  8.99 us
    all_gather x1, blocking collectives, on_device(): lax.all_gather(to_sixteen(value_rows), 'outer', axis=1, tiled=True)  8.95 us
    unnamed x29, local copies, waits for them, and re-layouts  8.46 us
    all_to_all x1, waiting for transfers between devices, on_device(): lax.all_to_all(mid_out, 'inner', split_axis=1, concat_axis=0, tiled=True)  8.09 us
    all_to_all x1, starting transfers between devices, on_device(): lax.all_to_all(to_items(queries), 'inner', split_axis=0, concat_axis=1, t...  6.35 us
    all_to_all x1, waiting for transfers between devices, on_device(): lax.all_to_all(to_items(key_rows), 'inner', split_axis=0, concat_axis=1,...  6.09 us
    all_to_all x1, waiting for transfers between devices, on_device(): lax.all_to_all(gathered_v, 'inner', split_axis=0, concat_axis=1, tiled=True)  5.8 us
  transfers between devices with their start and end apart: 9, of which 7 were waited for; matrix products, arithmetic and copies ran while one was open for 65% of the time, Pallas kernels for 0%

commit v1 on v0

--- a/solution.py
+++ b/solution.py
@@ -1,9 +1,12 @@
-from functools import reduce
+import math
+from functools import partial, reduce
 
 import jax
 import jax.numpy as jnp
 import numpy as np
 from jax import lax
+from jax.experimental import pallas as pl
+from jax.experimental.pallas import tpu as pltpu
 from jax.sharding import PartitionSpec as P
 
 HEADS = 16
@@ -209,10 +212,284 @@
     return combined.reshape(tokens, features)
 
 
+def fused_kernel(
+    dims, q_ref, k_ref, v_ref, out_ref, q_buf, k_buf, v_buf, far_k, far_v, pick_k, pick_v, ready,
+    in_send, in_recv, far_send, far_recv, back_send, back_recv, own_sem, own_back,
+):
+    inner, outer, tokens, slab, width, block = dims
+    group = tokens * inner
+    far_len = group // 4
+    per_slab = slab // width
+    me = lax.axis_index("inner")
+    mine = lax.axis_index("outer")
+    band = me * per_slab // 4
+    sources = (k_ref, v_ref, q_ref)
+    buffers = (k_buf, v_buf, q_buf)
+
+    def columns(index):
+        return pl.ds(pl.multiple_of(index * slab, slab), slab)
+
+    def rows(index):
+        return pl.ds(pl.multiple_of(index * tokens, tokens), tokens)
+
+    def inbound(which, peer, owner):
+        return pltpu.make_async_remote_copy(
+            src_ref=sources[which].at[:, columns(peer)],
+            dst_ref=buffers[which].at[rows(owner), :],
+            send_sem=in_send.at[which, peer],
+            recv_sem=in_recv.at[which, owner],
+            device_id={"inner": peer},
+            device_id_type=pl.DeviceIdType.MESH,
+        )
+
+    def farbound(which, peer, owner):
+        return pltpu.make_async_remote_copy(
+            src_ref=(pick_k, pick_v)[which],
+            dst_ref=(far_k, far_v)[which].at[owner],
+            send_sem=far_send.at[which, peer],
+            recv_sem=far_recv.at[which, owner],
+            device_id={"outer": peer},
+            device_id_type=pl.DeviceIdType.MESH,
+        )
+
+    def backbound(peer, owner):
+        return pltpu.make_async_remote_copy(
+            src_ref=ready.at[rows(peer), :],
+            dst_ref=out_ref.at[:, columns(owner)],
+            send_sem=back_send.at[peer],
+            recv_sem=back_recv.at[owner],
+            device_id={"inner": peer},
+            device_id_type=pl.DeviceIdType.MESH,
+        )
+
+    own_in = [
+        pltpu.make_async_copy(
+            sources[which].at[:, columns(me)], buffers[which].at[rows(me), :], own_sem.at[which]
+        )
+        for which in range(3)
+    ]
+    for copy in own_in:
+        copy.start()
+    barrier = pltpu.get_barrier_semaphore()
+    for step in range(1, inner):
+        pl.semaphore_signal(
+            barrier, inc=1, device_id={"inner": lax.rem(me + step, inner)},
+            device_id_type=pl.DeviceIdType.MESH,
+        )
+    for step in range(1, outer):
+        pl.semaphore_signal(
+            barrier, inc=1, device_id={"outer": lax.rem(mine + step, outer)},
+            device_id_type=pl.DeviceIdType.MESH,
+        )
+    pl.semaphore_wait(barrier, inner + outer - 2)
+
+    for which in range(3):
+        for step in range(1, inner):
+            inbound(which, lax.rem(me + step, inner), me).start()
+
+    for other in range(outer - 1):
+
+        @pl.when(mine <= other)
+        def _():
+            far_k[other] = jnp.zeros((far_len, slab), jnp.bfloat16)
+            far_v[other] = jnp.zeros((far_len, slab), jnp.bfloat16)
+
+    query_at = lax.broadcasted_iota(jnp.int32, (block, block), 0)
+    key_at = lax.broadcasted_iota(jnp.int32, (block, block), 1)
+    levels = (query_at % 4 == key_at % 4).astype(jnp.int32) + (
+        (query_at % 16 == key_at % 16) & (query_at % 16 // 4 == band)
+    ).astype(jnp.int32)
+
+    def log_count(count):
+        return jnp.where(
+            count == 0,
+            FLOOR_SCORE,
+            jnp.where(count == 1, 0.0, jnp.where(count == 2, 1.0, math.log2(3.0))),
+        )
+
+    below = log_count(levels)
+    diagonal = log_count(
+        jnp.where(
+            key_at <= query_at, levels + (query_at // tokens == key_at // tokens).astype(jnp.int32), 0
+        )
+    )
+    far_query = lax.broadcasted_iota(jnp.int32, (block, far_len), 0)
+    far_key = lax.broadcasted_iota(jnp.int32, (block, far_len), 1)
+    far_one = jnp.where(far_query % 16 == 4 * band + far_key % 4, 0.0, FLOOR_SCORE)
+    far_table = jnp.concatenate(
+        [jnp.where(other < mine, far_one, FLOOR_SCORE) for other in range(outer - 1)], axis=1
+    )
+    picked = lax.broadcasted_iota(jnp.int32, (far_len, group), 0)
+    picker = jnp.where(
+        lax.broadcasted_iota(jnp.int32, (far_len, group), 1)
+        == picked // 4 * 16 + 4 * band + picked % 4,
+        1.0,
+        0.0,
+    ).astype(jnp.bfloat16)
+
+    def arrive(which):
+        own_in[which].wait()
+        for step in range(1, inner):
+            inbound(which, me, lax.rem(me + step, inner)).wait_recv()
+
+    for which in range(2):
+        arrive(which)
+        (pick_k, pick_v)[which][...] = jnp.dot(
+            picker, buffers[which][...], preferred_element_type=jnp.float32
+        ).astype(jnp.bfloat16)
+        for other in range(1, outer):
+
+            @pl.when(mine < other)
+            def _():
+                farbound(which, other, mine).start()
+
+    arrive(2)
+    factor = width ** (-0.5) * math.log2(math.e)
+    lane_head = lax.broadcasted_iota(jnp.int32, (block, slab), 1) // width
+    contract = (((1,), (1,)), ((), ()))
+
+    def query_of(index, head):
+        piece = q_buf[index * block : (index + 1) * block, :]
+        return jnp.where(lane_head == head, piece, jnp.zeros_like(piece))
+
+    states = []
+    for index in range(group // block):
+        reach = (index + 1) * block
+        table = jnp.concatenate([below] * index + [diagonal], axis=1)
+        for head in range(per_slab):
+            scores = lax.dot_general(
+                query_of(index, head), k_buf[:reach, :], contract,
+                preferred_element_type=jnp.float32,
+            )
+            scores = scores * factor + table
+            top = jnp.max(scores, axis=1, keepdims=True)
+            weights = jnp.exp2(scores - top)
+            total = jnp.sum(weights, axis=1, keepdims=True)
+            summed = jnp.dot(
+                weights.astype(jnp.bfloat16), v_buf[:reach, :], preferred_element_type=jnp.float32
+            )
+            states.append((top, total, summed))
+
+    for other in range(outer - 1):
+
+        @pl.when(mine > other)
+        def _():
+            farbound(0, mine, other).wait_recv()
+            farbound(1, mine, other).wait_recv()
+
+    far_keys = far_k[...].reshape((outer - 1) * far_len, slab)
+    far_values = far_v[...].reshape((outer - 1) * far_len, slab)
+    for index in range(group // block):
+        result = None
+        for head in range(per_slab):
+            top, total, summed = states[index * per_slab + head]
+            scores = lax.dot_general(
+                query_of(index, head), far_keys, contract, preferred_element_type=jnp.float32
+            )
+            scores = scores * factor + far_table
+            new_top = jnp.maximum(top, jnp.max(scores, axis=1, keepdims=True))
+            rescale = jnp.exp2(top - new_top)
+            weights = jnp.exp2(scores - new_top)
+            total = total * rescale + jnp.sum(weights, axis=1, keepdims=True)
+            summed = summed * rescale + jnp.dot(
+                weights.astype(jnp.bfloat16), far_values, preferred_element_type=jnp.float32
+            )
+            finished = summed / total
+            result = finished if result is None else jnp.where(lane_head == head, finished, result)
+        ready[index * block : (index + 1) * block, :] = result
+        for peer in range(index * block // tokens, (index + 1) * block // tokens):
+
+            @pl.when(me != peer)
+            def _():
+                backbound(peer, me).start()
+
+            @pl.when(me == peer)
+            def _():
+                pltpu.make_async_copy(
+                    ready.at[rows(peer), :], out_ref.at[:, columns(peer)], own_back
+                ).start()
+
+    for step in range(1, inner):
+        backbound(me, lax.rem(me + step, inner)).wait_recv()
+    pltpu.make_async_copy(ready.at[rows(me), :], out_ref.at[:, columns(me)], own_back).wait()
+    for step in range(1, inner):
+        peer = lax.rem(me + step, inner)
+        for which in range(3):
+            inbound(which, peer, me).wait_send()
+        backbound(peer, me).wait_send()
+    for other in range(1, outer):
+
+        @pl.when(mine < other)
+        def _():
+            farbound(0, other, mine).wait_send()
+            farbound(1, other, mine).wait_send()
+
+
+def fused(queries, key_rows, value_rows, block):
+    tokens, features = queries.shape
+    inner = lax.axis_size("inner")
+    outer = lax.axis_size("outer")
+    slab = features // inner
+    group = tokens * inner
+    far_len = group // 4
+    any_space = pl.BlockSpec(memory_space=pl.ANY)
+    dims = (inner, outer, tokens, slab, features // HEADS, block)
+    return pl.pallas_call(
+        partial(fused_kernel, dims),
+        out_shape=jax.ShapeDtypeStruct((tokens, features), jnp.float32),
+        in_specs=[any_space] * 3,
+        out_specs=any_space,
+        scratch_shapes=[
+            pltpu.VMEM((group, slab), jnp.bfloat16),
+            pltpu.VMEM((group, slab), jnp.bfloat16),
+            pltpu.VMEM((group, slab), jnp.bfloat16),
+            pltpu.VMEM((outer - 1, far_len, slab), jnp.bfloat16),
+            pltpu.VMEM((outer - 1, far_len, slab), jnp.bfloat16),
+            pltpu.VMEM((far_len, slab), jnp.bfloat16),
+            pltpu.VMEM((far_len, slab), jnp.bfloat16),
+            pltpu.VMEM((group, slab), jnp.float32),
+            pltpu.SemaphoreType.DMA((3, inner)),
+            pltpu.SemaphoreType.DMA((3, inner)),
+            pltpu.SemaphoreType.DMA((2, outer)),
+            pltpu.SemaphoreType.DMA((2, outer)),
+            pltpu.SemaphoreType.DMA((inner,)),
+            pltpu.SemaphoreType.DMA((inner,)),
+            pltpu.SemaphoreType.DMA((3,)),
+            pltpu.SemaphoreType.DMA,
+        ],
+        compiler_params=pltpu.CompilerParams(collective_id=0, has_side_effects=True),
+    )(queries, key_rows, value_rows)
+
+
+def device_program(queries, key_rows, value_rows):
+    tokens, features = queries.shape
+    inner = lax.axis_size("inner")
+    outer = lax.axis_size("outer")
+    group = tokens * inner
+    block = 2 * tokens
+    slab = features // inner
+    per_slab = HEADS // inner
+    fits = (
+        HEADS % inner == 0
+        and outer > 1
+        and inner > 1
+        and per_slab > 0
+        and 4 % max(per_slab, 1) == 0
+        and slab % 128 == 0
+        and tokens % 16 == 0
+        and group % block == 0
+        and group <= 1024
+        and (outer - 1) * group // 4 <= 1024
+    )
+    if fits:
+        return fused(queries, key_rows, value_rows, block)
+    return on_device(queries, key_rows, value_rows)
+
+
 def solution(mesh):
     placed = (P(("outer", "inner"), None), P(("outer", "inner"), None), P(("outer", "inner"), None))
     return jax.shard_map(
-        on_device,
+        device_program,
         mesh=mesh,
         in_specs=placed,
         out_specs=P(("outer", "inner"), None),

time: 283 us -> 26.6 us (0.09)
  the two profiles are of different devices: /device:TPU:0 before, /device:TPU:29 now
where the time goes in v1:
time: 26.6 us; the launch traced here: 26.5 us
  Pallas kernels  24.8 us (93%)
  local copies, waits for them, and re-layouts  1.67 us (6%)
    pallas_call x1, Pallas kernels, fused(): pl.pallas_call(partial(fused_kernel, dims), out_shape=jax.ShapeDtypeStruc...  24.8 us
    unnamed x1, local copies, waits for them, and re-layouts  1.67 us

profile of v1, /device:TPU:29, one launch (start us, length us, event | category | flops | bytes accessed | tf_op | source)
XLA Modules:
  0.0 26.5 jit_solution(1500571611842472384)
XLA Ops:
  0.0 24.8 %shard_map.37 = f32[64,1024]{1,0:T(8,128)} custom-call(bf16[64,1024]{1,0:T(8,128)(2,1)} %q_ref.1, bf16[64,1024]{1,0:T(8,128)(2,1)} %k_ref.1, bf16[64,1024]{1,0:T(8,128)(2,1)} %v_ref.1), custom_call_target="tpu_custom_call" | custom-call | tf_op jit(solution)/shard_map/pallas_call | solution.py:437
  24.8 1.7 %copy.5 = f32[64,1024]{1,0:T(8,128)} copy(f32[64,1024]{1,0:T(8,128)} %shard_map.37) | data formatting | bytes 524288

commit v2 on v1

--- a/solution.py
+++ b/solution.py
@@ -213,8 +213,8 @@
 
 
 def fused_kernel(
-    dims, q_ref, k_ref, v_ref, out_ref, q_buf, k_buf, v_buf, far_k, far_v, pick_k, pick_v, ready,
-    in_send, in_recv, far_send, far_recv, back_send, back_recv, own_sem, own_back,
+    dims, q_ref, k_ref, v_ref, out_ref, q_held, k_held, v_held, q_buf, k_buf, v_buf, far_k, far_v, pick_k, pick_v, ready, ready_half, landed,
+    in_send, in_recv, far_send, far_recv, back_send, back_recv, cross_send, cross_recv, own_sem, own_back, held_sem,
 ):
     inner, outer, tokens, slab, width, block = dims
     group = tokens * inner
@@ -224,6 +224,10 @@
     mine = lax.axis_index("outer")
     band = me * per_slab // 4
     sources = (k_ref, v_ref, q_ref)
+    held = (k_held, v_held, q_held)
+    half = inner // 2
+    blocks = group // block
+    order = [at for pair in zip(range(blocks // 2, blocks), range(blocks // 2)) for at in pair]
     buffers = (k_buf, v_buf, q_buf)
 
     def columns(index):
@@ -234,7 +238,7 @@
 
     def inbound(which, peer, owner):
         return pltpu.make_async_remote_copy(
-            src_ref=sources[which].at[:, columns(peer)],
+            src_ref=held[which].at[:, columns(peer)],
             dst_ref=buffers[which].at[rows(owner), :],
             send_sem=in_send.at[which, peer],
             recv_sem=in_recv.at[which, owner],
@@ -262,13 +266,29 @@
             device_id_type=pl.DeviceIdType.MESH,
         )
 
+    def crossbound(peer, owner):
+        return pltpu.make_async_remote_copy(
+            src_ref=ready_half.at[rows(peer), :],
+            dst_ref=landed.at[:, columns(owner)],
+            send_sem=cross_send.at[peer],
+            recv_sem=cross_recv.at[owner],
+            device_id={"inner": peer},
+            device_id_type=pl.DeviceIdType.MESH,
+        )
+
+    def near(peer):
+        return (me // half == peer // half) & (me != peer)
+
     own_in = [
         pltpu.make_async_copy(
             sources[which].at[:, columns(me)], buffers[which].at[rows(me), :], own_sem.at[which]
         )
         for which in range(3)
     ]
-    for copy in own_in:
+    own_held = [
+        pltpu.make_async_copy(sources[which], held[which], held_sem.at[which]) for which in range(3)
+    ]
+    for copy in own_held + own_in:
         copy.start()
     barrier = pltpu.get_barrier_semaphore()
     for step in range(1, inner):
@@ -284,6 +304,7 @@
     pl.semaphore_wait(barrier, inner + outer - 2)
 
     for which in range(3):
+        own_held[which].wait()
         for step in range(1, inner):
             inbound(which, lax.rem(me + step, inner), me).start()
 
@@ -343,7 +364,6 @@
             def _():
                 farbound(which, other, mine).start()
 
-    arrive(2)
     factor = width ** (-0.5) * math.log2(math.e)
     lane_head = lax.broadcasted_iota(jnp.int32, (block, slab), 1) // width
     contract = (((1,), (1,)), ((), ()))
@@ -352,8 +372,15 @@
         piece = q_buf[index * block : (index + 1) * block, :]
         return jnp.where(lane_head == head, piece, jnp.zeros_like(piece))
 
-    states = []
-    for index in range(group // block):
+    own_in[2].wait()
+    states = {}
+    for index in order:
+        for peer in range(index * block // tokens, (index + 1) * block // tokens):
+
+            @pl.when(me != peer)
+            def _():
+                inbound(2, me, peer).wait_recv()
+
         reach = (index + 1) * block
         table = jnp.concatenate([below] * index + [diagonal], axis=1)
         for head in range(per_slab):
@@ -368,7 +395,7 @@
             summed = jnp.dot(
                 weights.astype(jnp.bfloat16), v_buf[:reach, :], preferred_element_type=jnp.float32
             )
-            states.append((top, total, summed))
+            states[index, head] = (top, total, summed)
 
     for other in range(outer - 1):
 
@@ -379,10 +406,10 @@
 
     far_keys = far_k[...].reshape((outer - 1) * far_len, slab)
     far_values = far_v[...].reshape((outer - 1) * far_len, slab)
-    for index in range(group // block):
+    for index in order:
         result = None
         for head in range(per_slab):
-            top, total, summed = states[index * per_slab + head]
+            top, total, summed = states[index, head]
             scores = lax.dot_general(
                 query_of(index, head), far_keys, contract, preferred_element_type=jnp.float32
             )
@@ -397,9 +424,14 @@
             finished = summed / total
             result = finished if result is None else jnp.where(lane_head == head, finished, result)
         ready[index * block : (index + 1) * block, :] = result
+        ready_half[index * block : (index + 1) * block, :] = result.astype(jnp.bfloat16)
         for peer in range(index * block // tokens, (index + 1) * block // tokens):
 
-            @pl.when(me != peer)
+            @pl.when(me // half != peer // half)
+            def _():
+                crossbound(peer, me).start()
+
+            @pl.when(near(peer))
             def _():
                 backbound(peer, me).start()
 
@@ -409,14 +441,34 @@
                     ready.at[rows(peer), :], out_ref.at[:, columns(peer)], own_back
                 ).start()
 
-    for step in range(1, inner):
-        backbound(me, lax.rem(me + step, inner)).wait_recv()
+    for owner in range(inner):
+
+        @pl.when(me // half != owner // half)
+        def _():
+            crossbound(me, owner).wait_recv()
+            place = slice(owner * slab, (owner + 1) * slab)
+            out_ref[:, place] = landed[:, place].astype(jnp.float32)
+
+    for owner in range(inner):
+
+        @pl.when(near(owner))
+        def _():
+            backbound(me, owner).wait_recv()
+
     pltpu.make_async_copy(ready.at[rows(me), :], out_ref.at[:, columns(me)], own_back).wait()
     for step in range(1, inner):
         peer = lax.rem(me + step, inner)
         for which in range(3):
             inbound(which, peer, me).wait_send()
-        backbound(peer, me).wait_send()
+
+        @pl.when(me // half != peer // half)
+        def _():
+            crossbound(peer, me).wait_send()
+
+        @pl.when(near(peer))
+        def _():
+            backbound(peer, me).wait_send()
+
     for other in range(1, outer):
 
         @pl.when(mine < other)
@@ -436,10 +488,13 @@
     dims = (inner, outer, tokens, slab, features // HEADS, block)
     return pl.pallas_call(
         partial(fused_kernel, dims),
-        out_shape=jax.ShapeDtypeStruct((tokens, features), jnp.float32),
+        out_shape=pltpu.VMEM((tokens, features), jnp.float32),
         in_specs=[any_space] * 3,
-        out_specs=any_space,
+        out_specs=pl.BlockSpec(memory_space=pltpu.VMEM),
         scratch_shapes=[
+            pltpu.VMEM((tokens, features), jnp.bfloat16),
+            pltpu.VMEM((tokens, features), jnp.bfloat16),
+            pltpu.VMEM((tokens, features), jnp.bfloat16),
             pltpu.VMEM((group, slab), jnp.bfloat16),
             pltpu.VMEM((group, slab), jnp.bfloat16),
             pltpu.VMEM((group, slab), jnp.bfloat16),
@@ -448,14 +503,19 @@
             pltpu.VMEM((far_len, slab), jnp.bfloat16),
             pltpu.VMEM((far_len, slab), jnp.bfloat16),
             pltpu.VMEM((group, slab), jnp.float32),
+            pltpu.VMEM((group, slab), jnp.bfloat16),
+            pltpu.VMEM((tokens, features), jnp.bfloat16),
             pltpu.SemaphoreType.DMA((3, inner)),
             pltpu.SemaphoreType.DMA((3, inner)),
             pltpu.SemaphoreType.DMA((2, outer)),
             pltpu.SemaphoreType.DMA((2, outer)),
             pltpu.SemaphoreType.DMA((inner,)),
             pltpu.SemaphoreType.DMA((inner,)),
+            pltpu.SemaphoreType.DMA((inner,)),
+            pltpu.SemaphoreType.DMA((inner,)),
             pltpu.SemaphoreType.DMA((3,)),
             pltpu.SemaphoreType.DMA,
+            pltpu.SemaphoreType.DMA((3,)),
         ],
         compiler_params=pltpu.CompilerParams(collective_id=0, has_side_effects=True),
     )(queries, key_rows, value_rows)
@@ -472,12 +532,12 @@
     fits = (
         HEADS % inner == 0
         and outer > 1
-        and inner > 1
+        and inner % 2 == 0
         and per_slab > 0
         and 4 % max(per_slab, 1) == 0
         and slab % 128 == 0
         and tokens % 16 == 0
-        and group % block == 0
+        and group % (2 * block) == 0
         and group <= 1024
         and (outer - 1) * group // 4 <= 1024
     )

time: 26.6 us -> 24.5 us (0.921)
  the two profiles are of different devices: /device:TPU:29 before, /device:TPU:0 now
where the time goes in v2:
time: 24.5 us; the launch traced here: 24.4 us
  Pallas kernels  23.7 us (97%)
  local copies, waits for them, and re-layouts  0.71 us (3%)
    pallas_call x1, Pallas kernels, fused(): pl.pallas_call(partial(fused_kernel, dims), out_shape=pltpu.VMEM((tokens,...  23.7 us
    unnamed x1, local copies, waits for them, and re-layouts  0.71 us

profile of v2, /device:TPU:0, one launch (start us, length us, event | category | flops | bytes accessed | tf_op | source)
XLA Modules:
  0.0 24.4 jit_solution(11007554369347069159)
XLA Ops:
  0.0 23.7 %shard_map.37 = f32[64,1024]{1,0:T(8,128)S(1)} custom-call(bf16[64,1024]{1,0:T(8,128)(2,1)} %q_ref.1, bf16[64,1024]{1,0:T(8,128)(2,1)} %k_ref.1, bf16[64,1024]{1,0:T(8,128)(2,1)} %v_ref.1), custom_call_target="tpu_custom_call" | custom-call | tf_op jit(solution)/shard_map/pallas_call | solution.py:489
  23.7 0.7 %copy.5 = f32[64,1024]{1,0:T(8,128)} copy(f32[64,1024]{1,0:T(8,128)S(1)} %shard_map.37) | data formatting | bytes 524288

commit v3 on v2

--- a/solution.py
+++ b/solution.py
@@ -226,8 +226,7 @@
     sources = (k_ref, v_ref, q_ref)
     held = (k_held, v_held, q_held)
     half = inner // 2
-    blocks = group // block
-    order = [at for pair in zip(range(blocks // 2, blocks), range(blocks // 2)) for at in pair]
+    order = range(group // block)
     buffers = (k_buf, v_buf, q_buf)
 
     def columns(index):
@@ -537,7 +536,7 @@
         and 4 % max(per_slab, 1) == 0
         and slab % 128 == 0
         and tokens % 16 == 0
-        and group % (2 * block) == 0
+        and group % block == 0
         and group <= 1024
         and (outer - 1) * group // 4 <= 1024
     )

time: 24.5 us -> 23.5 us (0.959)
  Pallas kernels: 23.7 us -> 22.7 us
    pallas_call x1, Pallas kernels: 23.7 us -> 22.7 us  [fused(): pl.pallas_call(partial(fused_kernel, dims), out_shape=pltpu.VMEM((tokens,...]
where the time goes in v3:
time: 23.5 us; the launch traced here: 23.4 us
  Pallas kernels  22.7 us (97%)
  local copies, waits for them, and re-layouts  0.71 us (3%)
    pallas_call x1, Pallas kernels, fused(): pl.pallas_call(partial(fused_kernel, dims), out_shape=pltpu.VMEM((tokens,...  22.7 us
    unnamed x1, local copies, waits for them, and re-layouts  0.71 us

profile of v3, /device:TPU:0, one launch (start us, length us, event | category | flops | bytes accessed | tf_op | source)
XLA Modules:
  0.0 23.4 jit_solution(1402807498613888160)
XLA Ops:
  0.0 22.7 %shard_map.37 = f32[64,1024]{1,0:T(8,128)S(1)} custom-call(bf16[64,1024]{1,0:T(8,128)(2,1)} %q_ref.1, bf16[64,1024]{1,0:T(8,128)(2,1)} %k_ref.1, bf16[64,1024]{1,0:T(8,128)(2,1)} %v_ref.1), custom_call_target="tpu_custom_call" | custom-call | tf_op jit(solution)/shard_map/pallas_call | solution.py:488
  22.7 0.7 %copy.5 = f32[64,1024]{1,0:T(8,128)} copy(f32[64,1024]{1,0:T(8,128)S(1)} %shard_map.37) | data formatting | bytes 524288
